TPU v7x, 32 devices: a whole 2x2x4 slice. The times are simulated.
32 devices in a mesh: ctx: 8 (over z, x), fsdp: 4 (over y, core).
Axes of the slice: x: 2, y: 2, z: 4, core: 2. Of those that a mesh axis runs over, the one named last changes fastest.
Arguments:
- tokens: bfloat16 [8, 2, 256, 1536], P('ctx', None, 'fsdp'), may hold values from -6 to 6
- pairing: int32 [8], replicated, may hold values from 0 to 7, each once
- gain_attn: bfloat16 [1536], P('fsdp'), may hold values from 0.099609375 to 1.8984375
- w_qkv: bfloat16 [1536, 2048], P('fsdp'), may hold values from -0.15625 to 0.15625
- b_qkv: bfloat16 [2048], P('fsdp'), may hold values from -10 to 10
- w_out: bfloat16 [1536, 1536], P('fsdp'), may hold values from -0.625 to 0.625
- gain_mlp: bfloat16 [1536], P('fsdp'), may hold values from 0.099609375 to 1.8984375
- w_gate_up: bfloat16 [1536, 2, 4480], P('fsdp'), may hold values from -0.15625 to 0.15625
- w_down: bfloat16 [4480, 1536], P('fsdp'), may hold values from -0.09375 to 0.09375
- cotangent: bfloat16 [8, 2, 256, 1536], P('ctx', None, 'fsdp'), may hold values from -6 to 6
Outputs:
- block_output: bfloat16 [8, 2, 256, 1536], P('ctx', None, 'fsdp')
- d_tokens: float32 [8, 2, 256, 1536], P('ctx', None, 'fsdp')
- d_gain_attn: float32 [1536], P('fsdp')
- d_w_qkv: float32 [1536, 2048], P('fsdp')
- d_b_qkv: float32 [2048], P('fsdp')
- d_w_out: float32 [1536, 1536], P('fsdp')
- d_gain_mlp: float32 [1536], P('fsdp')
- d_w_gate_up: float32 [1536, 2, 4480], P('fsdp')
- d_w_down: float32 [4480, 1536], P('fsdp')
Inputs may be any that keep to these rules, and one draw needn't show every extreme that they name: Each index of ctx holds stretches pairing[c] and 2 * 8 - 1 - pairing[c] of the sequence.
All inputs are finite; a program needn't handle non-finite values.
Results may differ from a plain program's by a relative error of at most 0.02.
The roundings to bfloat16 on the way count: a program that leaves them out, or rounds other values in their place, can miss the bound.
Values may be sent and summed in bfloat16 or wider, within the bound.
A program may use at most 384 MiB of HBM per device.

v0:
```python
import jax
import jax.numpy as jnp
from jax import lax
from jax.sharding import PartitionSpec as P

D = 1536
HEADS = 12
KV_HEADS = 2
HEAD_DIM = 128
eps = 1e-06
rope_base = 1000000.0


def rope_tables(position):
    half = HEAD_DIM // 2
    inverse = rope_base ** (-(jnp.arange(half, dtype=jnp.float32) * 2.0 / HEAD_DIM))
    angle = position.astype(jnp.float32)[:, None] * inverse[None, :]
    return (jnp.cos(angle)[:, None, :], jnp.sin(angle)[:, None, :])


def rotate(vectors, cosines, sines):
    half = HEAD_DIM // 2
    first, second = (vectors[..., :half], vectors[..., half:])
    return jnp.concatenate([first * cosines - second * sines, second * cosines + first * sines], -1)


def unrotate(grads, cosines, sines):
    half = HEAD_DIM // 2
    first, second = (grads[..., :half], grads[..., half:])
    return jnp.concatenate([first * cosines + second * sines, second * cosines - first * sines], -1)


def rms_scale(values):
    return lax.rsqrt(jnp.mean(values * values, -1, keepdims=True) + eps)


def rms_backward(values, scale_rows, gain, d_normed):
    d_gain = jnp.sum(d_normed * values * scale_rows, 0)
    d_inner = d_normed * gain
    d_values = scale_rows * d_inner - values * scale_rows**3 * jnp.mean(
        d_inner * values, -1, keepdims=True
    )
    return (d_values, d_gain)


def contract_rows(left, right):
    return lax.dot_general(
        left, right, (((0,), (0,)), ((), ())), preferred_element_type=jnp.float32
    )


def contract_cols(left, right):
    return lax.dot_general(
        left, right, (((1,), (1,)), ((), ())), preferred_element_type=jnp.float32
    )


def body(tokens, pairing, gain_attn, w_qkv, b_qkv, w_out, gain_mlp, w_gate_up, w_down, cotangent):
    f32 = jnp.float32
    bf16 = jnp.bfloat16
    half_rows = tokens.shape[2]
    n_ctx = lax.axis_size("ctx")
    n_fsdp = lax.axis_size("fsdp")
    ctx_index = lax.axis_index("ctx")
    fsdp_index = lax.axis_index("fsdp")
    stretch_len = half_rows * n_fsdp
    everyone = n_ctx * n_fsdp
    sequence = 2 * n_ctx * stretch_len
    local_count = 2 * half_rows
    q_width = HEADS * HEAD_DIM
    kv_width = KV_HEADS * HEAD_DIM
    per_group = HEADS // KV_HEADS
    softmax_scale = HEAD_DIM ** (-0.5)
    owner_range = jnp.arange(n_ctx, dtype=jnp.int32)
    own_first = jnp.sum(jnp.where(owner_range == ctx_index, pairing, 0))
    own_second = 2 * n_ctx - 1 - own_first
    inverse_pair = jnp.sum(
        owner_range[:, None] * (pairing[:, None] == owner_range[None, :]).astype(jnp.int32), 0
    )
    offsets = fsdp_index * half_rows + jnp.arange(half_rows, dtype=jnp.int32)
    own_pos = jnp.concatenate(
        [own_first * stretch_len + offsets, own_second * stretch_len + offsets]
    )
    gain_one_w, w_qkv_full, b_qkv_full, w_out_full = (
        lax.all_gather(gain_attn, "fsdp", axis=0, tiled=True),
        lax.all_gather(w_qkv, "fsdp", axis=0, tiled=True),
        lax.all_gather(b_qkv, "fsdp", axis=0, tiled=True),
        lax.all_gather(w_out, "fsdp", axis=0, tiled=True),
    )
    gain_one = gain_one_w.astype(f32)
    inputs = tokens.reshape(local_count, D).astype(f32)
    scale_one = rms_scale(inputs)
    normed1 = (inputs * scale_one * gain_one).astype(bf16)
    qkv = jnp.dot(normed1, w_qkv_full, preferred_element_type=f32) + b_qkv_full.astype(f32)
    cosines, sines = rope_tables(own_pos)
    query16 = rotate(qkv[:, :q_width].reshape(local_count, HEADS, HEAD_DIM), cosines, sines).astype(
        bf16
    )
    key16 = rotate(
        qkv[:, q_width : q_width + kv_width].reshape(local_count, KV_HEADS, HEAD_DIM),
        cosines,
        sines,
    ).astype(bf16)
    value16 = qkv[:, q_width + kv_width :].astype(bf16)
    keys_gathered, values_gathered = (
        lax.all_gather(key16.reshape(2, half_rows, kv_width), ("ctx", "fsdp"), axis=1, tiled=True),
        lax.all_gather(
            value16.reshape(2, half_rows, kv_width), ("ctx", "fsdp"), axis=1, tiled=True
        ),
    )

    def by_position(gathered):
        laid = gathered.reshape(2, n_ctx, stretch_len, kv_width)
        ordered = jnp.concatenate(
            [
                jnp.take(laid[0], inverse_pair, axis=0),
                jnp.take(laid[1], inverse_pair[::-1], axis=0),
            ],
            0,
        )
        return ordered.reshape(sequence, KV_HEADS, HEAD_DIM)

    keys_sorted = by_position(keys_gathered)
    values_sorted = by_position(values_gathered)
    query_halves = query16.reshape(2, half_rows, KV_HEADS, per_group, HEAD_DIM)
    pos_halves = own_pos.reshape(2, half_rows)
    stretch_ids = (own_first, own_second)
    key_iota = jnp.arange(stretch_len, dtype=jnp.int32)

    def masked_scores(query_half, pos_half, key_block, start):
        scores = (
            jnp.einsum("tkgd,skd->kgts", query_half, key_block, preferred_element_type=f32)
            * softmax_scale
        )
        visible = (start + key_iota)[None, None, None, :] <= pos_half[None, None, :, None]
        return (jnp.where(visible, scores, -1e30), visible)

    lse_parts = []
    att_parts = []
    for which in range(2):
        forward_query_half = query_halves[which]
        forward_pos_half = pos_halves[which]
        forward_stretch_id = stretch_ids[which]

        def stat_step(block, carry):
            running_max, totals = carry
            start = block * stretch_len
            key_block = lax.dynamic_slice_in_dim(keys_sorted, start, stretch_len, 0)
            scores, visible = masked_scores(forward_query_half, forward_pos_half, key_block, start)
            new_max = jnp.maximum(running_max, jnp.max(scores, -1))
            weights = jnp.where(visible, jnp.exp(scores - new_max[..., None]), 0.0)
            totals = totals * jnp.exp(running_max - new_max) + jnp.sum(weights, -1)
            return (new_max, totals)

        start_max = jnp.full((KV_HEADS, per_group, half_rows), -1e30, f32)
        start_tot = jnp.zeros((KV_HEADS, per_group, half_rows), f32)
        running_max, totals = lax.fori_loop(
            0, forward_stretch_id + 1, stat_step, (start_max, start_tot)
        )
        lse_half = running_max + jnp.log(totals)

        def value_step(block, accumulated):
            start = block * stretch_len
            key_block = lax.dynamic_slice_in_dim(keys_sorted, start, stretch_len, 0)
            value_block = lax.dynamic_slice_in_dim(values_sorted, start, stretch_len, 0)
            scores, visible = masked_scores(forward_query_half, forward_pos_half, key_block, start)
            probs16 = jnp.where(visible, jnp.exp(scores - lse_half[..., None]), 0.0).astype(bf16)
            return accumulated + jnp.einsum(
                "kgts,skd->kgtd", probs16, value_block, preferred_element_type=f32
            )

        start_acc = jnp.zeros((KV_HEADS, per_group, half_rows, HEAD_DIM), f32)
        accumulated = lax.fori_loop(0, forward_stretch_id + 1, value_step, start_acc)
        lse_half, accumulated = (lse_half, accumulated)
        lse_parts.append(lse_half)
        att_parts.append(accumulated)
    attended = jnp.concatenate(att_parts, 2)
    attended16 = attended.transpose(2, 0, 1, 3).reshape(local_count, q_width).astype(bf16)
    hidden = inputs + jnp.dot(attended16, w_out_full, preferred_element_type=f32)
    gain_two_w, w_gu_full, w_down_full = (
        lax.all_gather(gain_mlp, "fsdp", axis=0, tiled=True),
        lax.all_gather(w_gate_up, "fsdp", axis=0, tiled=True),
        lax.all_gather(w_down, "fsdp", axis=0, tiled=True),
    )
    gain_two = gain_two_w.astype(f32)
    scale_two = rms_scale(hidden)
    normed2 = (hidden * scale_two * gain_two).astype(bf16)
    gate_up = jnp.einsum("td,def->tef", normed2, w_gu_full, preferred_element_type=f32)
    gate_val = gate_up[:, 0]
    up_val = gate_up[:, 1]
    act16 = (jax.nn.silu(gate_val) * up_val).astype(bf16)
    result = hidden + jnp.dot(act16, w_down_full, preferred_element_type=f32)
    block_output = result.astype(bf16).reshape(tokens.shape)
    gain_two_back, w_gu_back, w_down_back = (
        lax.all_gather(gain_mlp, "fsdp", axis=0, tiled=True),
        lax.all_gather(w_gate_up, "fsdp", axis=0, tiled=True),
        lax.all_gather(w_down, "fsdp", axis=0, tiled=True),
    )
    cot = cotangent.reshape(local_count, D)
    d_act = contract_cols(cot, w_down_back)
    d_w_down = contract_rows(act16, cot)
    sigmoid_gate = jax.nn.sigmoid(gate_val)
    d_gate = d_act * up_val * sigmoid_gate * (1.0 + gate_val * (1.0 - sigmoid_gate))
    d_up = d_act * gate_val * sigmoid_gate
    d_gu16 = jnp.stack([d_gate, d_up], 1).astype(bf16)
    d_w_gate_up = jnp.einsum("td,tef->def", normed2, d_gu16, preferred_element_type=f32)
    d_normed2 = jnp.einsum("tef,def->td", d_gu16, w_gu_back, preferred_element_type=f32)
    d_hidden_norm, d_gain_two = rms_backward(
        hidden, scale_two, gain_two_back.astype(f32), d_normed2
    )
    mlp_shards = (
        lax.psum_scatter(d_gain_two, "fsdp", scatter_dimension=0, tiled=True),
        lax.psum_scatter(d_w_gate_up, "fsdp", scatter_dimension=0, tiled=True),
        lax.psum_scatter(d_w_down, "fsdp", scatter_dimension=0, tiled=True),
    )
    gain_two_shard, gate_up_shard, down_shard = mlp_shards
    d_gain_mlp, d_w_gate_up_out, d_w_down_out = lax.psum(
        (gain_two_shard, gate_up_shard, down_shard), "ctx"
    )
    d_hidden = cot.astype(f32) + d_hidden_norm
    d_hidden16 = d_hidden.astype(bf16)
    gain_one_back, w_qkv_back, b_unused, w_out_back = (
        lax.all_gather(gain_attn, "fsdp", axis=0, tiled=True),
        lax.all_gather(w_qkv, "fsdp", axis=0, tiled=True),
        lax.all_gather(b_qkv, "fsdp", axis=0, tiled=True),
        lax.all_gather(w_out, "fsdp", axis=0, tiled=True),
    )
    d_w_out = contract_rows(attended16, d_hidden16)
    d_attended16 = contract_cols(d_hidden16, w_out_back).astype(bf16)
    delta = jnp.sum(
        d_attended16.astype(f32).reshape(local_count, HEADS, HEAD_DIM)
        * attended16.astype(f32).reshape(local_count, HEADS, HEAD_DIM),
        -1,
    )
    delta = delta.reshape(local_count, KV_HEADS, per_group).transpose(1, 2, 0)
    d_att_halves = d_attended16.reshape(2, half_rows, KV_HEADS, per_group, HEAD_DIM)
    zero_kv = jnp.zeros((sequence, KV_HEADS, HEAD_DIM), f32)
    buffers = (zero_kv, zero_kv)
    dq_parts = []
    for which in range(2):
        span = slice(which * half_rows, (which + 1) * half_rows)
        backward_query_half = query_halves[which]
        backward_pos_half = pos_halves[which]
        backward_lse_half = lse_parts[which]
        delta_half = delta[:, :, span]
        d_att_half = d_att_halves[which]

        def step(block, carry):
            d_query, d_key_buf, d_value_buf = carry
            start = block * stretch_len
            key_block = lax.dynamic_slice_in_dim(keys_sorted, start, stretch_len, 0)
            value_block = lax.dynamic_slice_in_dim(values_sorted, start, stretch_len, 0)
            scores, visible = masked_scores(
                backward_query_half, backward_pos_half, key_block, start
            )
            probs = jnp.where(visible, jnp.exp(scores - backward_lse_half[..., None]), 0.0)
            probs16 = probs.astype(bf16)
            d_probs = jnp.einsum(
                "tkgd,skd->kgts", d_att_half, value_block, preferred_element_type=f32
            )
            d_scores16 = (probs * (d_probs - delta_half[..., None])).astype(bf16)
            d_query = d_query + softmax_scale * jnp.einsum(
                "kgts,skd->kgtd", d_scores16, key_block, preferred_element_type=f32
            )
            d_key_block = softmax_scale * jnp.einsum(
                "kgts,tkgd->skd", d_scores16, backward_query_half, preferred_element_type=f32
            )
            d_value_block = jnp.einsum(
                "kgts,tkgd->skd", probs16, d_att_half, preferred_element_type=f32
            )
            d_key_buf = lax.dynamic_update_slice_in_dim(
                d_key_buf,
                lax.dynamic_slice_in_dim(d_key_buf, start, stretch_len, 0) + d_key_block,
                start,
                0,
            )
            d_value_buf = lax.dynamic_update_slice_in_dim(
                d_value_buf,
                lax.dynamic_slice_in_dim(d_value_buf, start, stretch_len, 0) + d_value_block,
                start,
                0,
            )
            return (d_query, d_key_buf, d_value_buf)

        zero_query = jnp.zeros((KV_HEADS, per_group, half_rows, HEAD_DIM), f32)
        d_query_half, d_key_buf, d_value_buf = lax.fori_loop(
            0, stretch_ids[which] + 1, step, (zero_query, buffers[0], buffers[1])
        )
        buffers = (d_key_buf, d_value_buf)
        dq_parts.append(d_query_half)
    d_query = jnp.concatenate(dq_parts, 2)

    def by_device(buffer):
        laid = buffer.reshape(2 * n_ctx, stretch_len, kv_width)
        ordered = jnp.stack(
            [jnp.take(laid, pairing, axis=0), jnp.take(laid, 2 * n_ctx - 1 - pairing, axis=0)], 0
        )
        return ordered.reshape(2, everyone * half_rows, kv_width)

    d_keys_own, d_values_own = (
        lax.psum_scatter(by_device(buffers[0]), ("ctx", "fsdp"), scatter_dimension=1, tiled=True),
        lax.psum_scatter(by_device(buffers[1]), ("ctx", "fsdp"), scatter_dimension=1, tiled=True),
    )
    d_query = unrotate(
        d_query.transpose(2, 0, 1, 3).reshape(local_count, HEADS, HEAD_DIM), cosines, sines
    ).reshape(local_count, q_width)
    d_keys = unrotate(d_keys_own.reshape(local_count, KV_HEADS, HEAD_DIM), cosines, sines).reshape(
        local_count, kv_width
    )
    d_qkv = jnp.concatenate([d_query, d_keys, d_values_own.reshape(local_count, kv_width)], 1)
    d_b_qkv = jnp.sum(d_qkv, 0)
    d_qkv16 = d_qkv.astype(bf16)
    d_w_qkv = contract_rows(normed1, d_qkv16)
    d_normed1 = contract_cols(d_qkv16, w_qkv_back)
    d_input_norm, d_gain_one = rms_backward(inputs, scale_one, gain_one_back.astype(f32), d_normed1)
    attn_shards = (
        lax.psum_scatter(d_gain_one, "fsdp", scatter_dimension=0, tiled=True),
        lax.psum_scatter(d_w_qkv, "fsdp", scatter_dimension=0, tiled=True),
        lax.psum_scatter(d_b_qkv, "fsdp", scatter_dimension=0, tiled=True),
        lax.psum_scatter(d_w_out, "fsdp", scatter_dimension=0, tiled=True),
    )
    gain_one_shard, qkv_shard, bias_shard, out_shard = attn_shards
    d_gain_attn, d_w_qkv_out, d_b_qkv_out, d_w_out_out = lax.psum(
        (gain_one_shard, qkv_shard, bias_shard, out_shard), "ctx"
    )
    d_tokens = (d_hidden + d_input_norm).reshape(tokens.shape)
    return (
        block_output,
        d_tokens,
        d_gain_attn,
        d_w_qkv_out,
        d_b_qkv_out,
        d_w_out_out,
        d_gain_mlp,
        d_w_gate_up_out,
        d_w_down_out,
    )


def solution(mesh):
    placed = (
        P("ctx", None, "fsdp", None),
        P(),
        P("fsdp"),
        P("fsdp", None),
        P("fsdp"),
        P("fsdp", None),
        P("fsdp"),
        P("fsdp", None, None),
        P("fsdp", None),
        P("ctx", None, "fsdp", None),
    )
    return jax.shard_map(
        body,
        mesh=mesh,
        in_specs=placed,
        out_specs=(
            P("ctx", None, "fsdp", None),
            P("ctx", None, "fsdp", None),
            P("fsdp"),
            P("fsdp", None),
            P("fsdp"),
            P("fsdp", None),
            P("fsdp"),
            P("fsdp", None, None),
            P("fsdp", None),
        ),
        check_vma=False,
    )
```

profile of v0, /device:TPU:0, one launch (start us, length us, event | category | flops | bytes accessed | tf_op | source)
XLA Modules:
  0.0 2571.1 jit_solution(16829387691928757474)
XLA Ops:
  8.7 6.2 all-gather
  16.8 5.5 all-gather.1
  22.5 36.2 %all-gather.10.cloned.1.call-done = bf16[1536,2048]{1,0:T(8,128)(2,1)} async-done(((bf16[384,2048]{1,0:T(8,128)(2,1)}), bf16[1536,2048]{1,0:T(8,128)(2,1)}) %all-gather.10.cloned.1.call-update) | async-done | bytes 6291472 | tf_op jit(solution)/shard_map/all_gather | solution.py:86
  58.7 3.8 convolution_add_fusion.2
  67.6 6.6 copy.160
  75.7 5.2 all-gather.2
  84.4 35.4 %all-gather.14.cloned.1.call-done = bf16[2,2048,256]{2,1,0:T(8,128)(2,1)} async-done(((bf16[2,64,256]{2,1,0:T(8,128)(2,1)}), bf16[2,2048,256]{2,1,0:T(8,128)(2,1)}) %all-gather.14.cloned.1.call-update) | async-done | bytes 2097168 | tf_op jit(solution)/shard_map/all_gather | solution.py:107
  123.0 55.6 %all-gather.12.cloned.1.call-done = bf16[2,2048,256]{2,1,0:T(8,128)(2,1)} async-done(((bf16[2,64,256]{2,1,0:T(8,128)(2,1)}), bf16[2,2048,256]{2,1,0:T(8,128)(2,1)}) %all-gather.12.cloned.1.call-update) | async-done | bytes 2097168 | tf_op jit(solution)/shard_map/all_gather | solution.py:106
  184.8 2.9 gather_fusion
  197.6 4.0 reshape.621
  201.5 3.2 copy.152
  204.7 13.9 while.80
  218.6 25.0 while.81
  250.4 3.4 multiply_reduce_fusion.2
  253.8 131.9 %all-gather.18.cloned.1.call-done = bf16[1536,2,4480]{2,0,1:T(8,128)(2,1)} async-done(((bf16[384,2,4480]{2,0,1:T(8,128)(2,1)}), bf16[1536,2,4480]{2,0,1:T(8,128)(2,1)}) %all-gather.18.cloned.1.call-update) | async-done | bytes 27525136 | tf_op jit(solution)/shard_map/all_gather | solution.py:182
  385.7 16.4 fusion.167
  402.1 73.9 %all-gather.20.cloned.1.call-done = bf16[4480,1536]{1,0:T(8,128)(2,1)} async-done(((bf16[1120,1536]{1,0:T(8,128)(2,1)}), bf16[4480,1536]{1,0:T(8,128)(2,1)}) %all-gather.20.cloned.1.call-update) | async-done | bytes 13762576 | tf_op jit(solution)/shard_map/all_gather | solution.py:183
  476.0 11.9 fusion.149
  487.8 16.1 multiply_reduce_fusion
  505.3 4.3 convolution_convert_fusion
  516.9 7.8 while.82
  525.0 123.9 %while.83 = (s32[]{:T(128)}, f32[2,6,64,128]{3,2,1,0:T(8,128)S(1)}, f32[4096,2,128]{2,0,1:T(8,128)}, f32[4096,2,128]{2,0,1:T(8,128)}, s32[]{:T(128)}, /*index=5*...) while((s32[]{:T(128)}, f32[2,6,64,128]{3,2,1,0:T(8,128)S(1)}, ...), condition=%wide.region_21.23_spmd.clone, body=%wide.region_20.22_spmd.clone.sunk | while | flops 253641088 | bytes 6595315 | solution.py:286
  648.9 9.1 copy.209
  658.0 6.4 reshape.625
  664.4 8.7 copy.211
  673.1 6.5 reshape.626
  679.6 4.3 gather_fusion.5
  683.9 4.3 gather_fusion.7
  688.2 4.3 gather_fusion.4
  692.5 4.3 gather_fusion.6
  696.8 4.2 broadcast_select_fusion.2
  705.2 4.5 pad_maximum_fusion
  709.8 5.0 fusion.163
  715.8 131.8 %reduce-scatter.9.cloned.1.call-done = f32[2,64,256]{2,1,0:T(8,128)} async-done(((f32[2,2048,256]{2,1,0:T(8,128)}), f32[2,64,256]{2,1,0:T(8,128)}) %reduce-scatter.9.cloned.1.call-update) | async-done | bytes 131088 | tf_op jit(solution)/shard_map/reduce_scatter | solution.py:302
  848.5 139.4 %reduce-scatter.7.cloned.1.call-done = f32[2,64,256]{2,1,0:T(8,128)} async-done(((f32[2,2048,256]{2,1,0:T(8,128)}), f32[2,64,256]{2,1,0:T(8,128)}) %reduce-scatter.7.cloned.1.call-update) | async-done | bytes 131088 | tf_op jit(solution)/shard_map/reduce_scatter | solution.py:301
  989.5 8.6 fusion.176
  999.2 14.8 fusion.145
  1015.3 23.1 fusion.143
  1038.5 25.8 %reduce-scatter.13.cloned.1.call-done = f32[384,1536]{1,0:T(8,128)} async-done(((f32[1536,1536]{1,0:T(8,128)}), f32[384,1536]{1,0:T(8,128)}) %reduce-scatter.13.cloned.1.call-update) | async-done | bytes 2359312 | tf_op jit(solution)/shard_map/reduce_scatter | solution.py:320
  1064.3 102.6 %reduce-scatter.11.cloned.1.call-done = f32[384,2048]{1,0:T(8,128)} async-done(((f32[1536,2048]{1,0:T(8,128)}), f32[384,2048]{1,0:T(8,128)}) %reduce-scatter.11.cloned.1.call-update) | async-done | bytes 3145744 | tf_op jit(solution)/shard_map/reduce_scatter | solution.py:318
  1167.0 200.4 %reduce-scatter.17.cloned.1.call-done = f32[1120,1536]{1,0:T(8,128)} async-done(((f32[4480,1536]{1,0:T(8,128)}), f32[1120,1536]{1,0:T(8,128)}) %reduce-scatter.17.cloned.1.call-update) | async-done | bytes 6881296 | tf_op jit(solution)/shard_map/reduce_scatter | solution.py:214
  1367.3 380.5 %reduce-scatter.15.cloned.1.call-done = f32[384,2,4480]{2,0,1:T(8,128)} async-done(((f32[1536,2,4480]{2,0,1:T(8,128)}), f32[384,2,4480]{2,0,1:T(8,128)}) %reduce-scatter.15.cloned.1.call-update) | async-done | bytes 13762576 | tf_op jit(solution)/shard_map/reduce_scatter | solution.py:213
  1750.9 9.4 fusion.132
  1760.7 3.7 fusion.159
  1764.5 11.6 all-reduce.5
  1776.3 23.8 all-reduce.3
  1803.1 720.3 %all-reduce.8.cloned.1.call-done = (f32[384,2048]{1,0:T(8,128)}, f32[384,1536]{1,0:T(8,128)}, f32[384,2,4480]{2,0,1:T(8,128)}, f32[1120,1536]{1,0:T(8,128)}) async-done(((f32[384,2048]{1,0:T(8,128)}, f32[384,1536]{1,0:T(8,128)}, f32[384,2,4480]{2,0,1:T(8,128)}, f32[1120,1536]{1,0:T(8,128)}), (f32[384,2048]{1,0:T(8,128)}, f32[384,1536]{1,0:T(8,128)}, f32[384,2,4480]{2,0,1:T(8,128)}, ...) | async-done | bytes 26148880 | tf_op jit(solution)/shard_map/psum | solution.py:323
  2523.4 33.1 %copy.180 = f32[384,2,4480]{2,1,0:T(2,128)} copy(f32[384,2,4480]{2,0,1:T(8,128)} %get-tuple-element.961) | data formatting | bytes 27525120
  (556 shorter events, 239.2 us)
Async XLA Ops:
  7.2 15.1 copy-start.5
  7.2 51.5 %all-gather.10.cloned.1.call-start = ((), (), s32[]{:S(2)}) async-start(), calls=%async_computation.6 | async-start | bytes 7864320 | tf_op jit(solution)/shard_map/all_gather | solution.py:86
  7.9 111.9 %all-gather.14.cloned.1.call-start = ((), (), s32[]{:S(2)}) async-start(), calls=%async_computation.8 | async-start | bytes 2162688 | tf_op jit(solution)/shard_map/all_gather | solution.py:107
  14.9 43.8 %copy-start.28 = (f32[1536]{0:T(1024)}, f32[1536]{0:T(1024)S(1)}, u32[]{:S(2)}) copy-start(f32[1536]{0:T(1024)S(1)} %reshape.584) | copy-start | bytes 18436
  16.1 42.6 %copy-start.32 = (f32[128]{0:T(128)}, f32[128]{0:T(128)S(1)}, u32[]{:S(2)}) copy-start(f32[128]{0:T(128)S(1)} %rsqrt.26) | copy-start | bytes 1540
  22.5 40.0 %copy-start.11 = (bf16[128,1536]{1,0:T(8,128)(2,1)}, bf16[128,1536]{1,0:T(8,128)(2,1)S(1)}, u32[]{:S(2)}) copy-start(bf16[128,1536]{1,0:T(8,128)(2,1)S(1)} %fusion.153) | copy-start | bytes 1179652
  58.7 4.5 copy-start.37
  63.1 115.5 %all-gather.12.cloned.1.call-start = ((), (), s32[]{:S(2)}) async-start(), calls=%async_computation.7 | async-start | bytes 2162688 | tf_op jit(solution)/shard_map/all_gather | solution.py:106
  65.5 18.3 copy-start.24
  65.5 18.3 copy-start.26
  65.7 8.5 copy-start.22
  67.0 183.5 %all-gather.16.cloned.1.call-start = ((), (), s32[]{:S(2)}) async-start(), calls=%async_computation.9 | async-start | bytes 5898240 | tf_op jit(solution)/shard_map/all_gather | solution.py:88
  67.5 318.2 %all-gather.18.cloned.1.call-start = ((), (), s32[]{:S(2)}) async-start(), calls=%async_computation.10 | async-start | bytes 34406400 | tf_op jit(solution)/shard_map/all_gather | solution.py:182
  74.2 401.7 %all-gather.20.cloned.1.call-start = ((), (), s32[]{:S(2)}) async-start(), calls=%async_computation.11 | async-start | bytes 17203200 | tf_op jit(solution)/shard_map/all_gather | solution.py:183
  74.8 772.7 %reduce-scatter.9.cloned.1.call-start = ((), (), s32[]{:S(2)}) async-start(), calls=%async_computation.13 | async-start | bytes 4325376 | tf_op jit(solution)/shard_map/reduce_scatter | solution.py:302
  187.7 2.8 copy-start.13
  193.9 2.0 copy-start.14
  193.9 2.2 copy-start.15
  247.2 3.2 copy-start.4
  247.2 6.5 copy-start.30
  385.7 90.2 %copy-start.18 = (bf16[1,2,64,1536]{3,2,1,0:T(8,128)(2,1)S(1)}, bf16[1,2,64,1536]{3,2,1,0:T(8,128)(2,1)}, u32[]{:S(2)}) copy-start(bf16[1,2,64,1536]{3,2,1,0:T(8,128)(2,1)} %param.35) | copy-start | bytes 1179652
  487.8 16.1 copy-start.20
  505.3 204.5 %copy-start.2 = (f32[128,1536]{1,0:T(8,128)}, f32[128,1536]{1,0:T(8,128)S(1)}, u32[]{:S(2)}) copy-start(f32[128,1536]{1,0:T(8,128)S(1)} %subtract_add_fusion) | copy-start | bytes 2359300
  514.6 2.3 copy-start.31
  692.5 4.3 copy-start.36
  696.8 4.2 copy-start.7
  696.8 4.2 copy-start.8
  696.8 4.2 copy-start.35
  705.2 282.7 %reduce-scatter.7.cloned.1.call-start = ((), (), s32[]{:S(2)}) async-start(), calls=%async_computation.12 | async-start | bytes 4325376 | tf_op jit(solution)/shard_map/reduce_scatter | solution.py:301
  709.7 354.6 %reduce-scatter.13.cloned.1.call-start = ((), (), s32[]{:S(2)}) async-start(), calls=%async_computation.15 | async-start | bytes 11796480 | tf_op jit(solution)/shard_map/reduce_scatter | solution.py:320
  714.8 452.1 %reduce-scatter.11.cloned.1.call-start = ((), (), s32[]{:S(2)}) async-start(), calls=%async_computation.14 | async-start | bytes 15728640 | tf_op jit(solution)/shard_map/reduce_scatter | solution.py:318
  714.9 273.9 %copy-start.23 = (f32[128,64]{1,0:T(8,128)S(1)}, f32[128,64]{1,0:T(8,128)}, u32[]{:S(2)}) copy-start(f32[128,64]{1,0:T(8,128)} %copy-done.22) | copy-start | bytes 98308
  715.6 273.9 %copy-start.12 = (bf16[128,1536]{1,0:T(8,128)(2,1)S(1)}, bf16[128,1536]{1,0:T(8,128)(2,1)}, u32[]{:S(2)}) copy-start(bf16[128,1536]{1,0:T(8,128)(2,1)} %copy-done.11) | copy-start | bytes 1179652
  715.8 282.3 %copy-start = (f32[128,12,128]{0,2,1:T(8,128)}, f32[128,12,128]{0,2,1:T(8,128)S(1)}, u32[]{:S(2)}) copy-start(f32[128,12,128]{0,2,1:T(8,128)S(1)} %pad_maximum_fusion.8) | copy-start | bytes 2359300
  998.1 369.2 %reduce-scatter.17.cloned.1.call-start = ((), (), s32[]{:S(2)}) async-start(), calls=%async_computation.17 | async-start | bytes 34406400 | tf_op jit(solution)/shard_map/reduce_scatter | solution.py:214
  1014.1 733.8 %reduce-scatter.15.cloned.1.call-start = ((), (), s32[]{:S(2)}) async-start(), calls=%async_computation.16 | async-start | bytes 68812800 | tf_op jit(solution)/shard_map/reduce_scatter | solution.py:213
  1038.5 1485.0 %all-reduce.8.cloned.1.call-start = ((), (), s32[]{:S(2)}) async-start(), calls=%async_computation.18 | async-start | bytes 52297728 | tf_op jit(solution)/shard_map/psum | solution.py:323
  1747.8 2.5 copy-start.33
  1747.8 12.8 slice-start
  1750.9 9.4 copy-start.1
  1750.9 9.8 slice-start.1
  1750.9 9.8 copy-start.6
  1750.9 9.8 copy-start.29
  1750.9 9.8 copy-start.34
  1760.7 40.0 %copy-start.3 = (f32[128,1536]{1,0:T(8,128)S(1)}, f32[128,1536]{1,0:T(8,128)}, u32[]{:S(2)}) copy-start(f32[128,1536]{1,0:T(8,128)} %copy-done.2) | copy-start | bytes 2359300
  2523.4 33.1 %copy-start.16 = (f32[384,2048]{1,0:T(8,128)S(1)}, f32[384,2048]{1,0:T(8,128)}, u32[]{:S(2)}) copy-start(f32[384,2048]{1,0:T(8,128)} %get-tuple-element.1648) | copy-start | bytes 9437188
  2523.4 34.8 %copy-start.17 = (f32[384,1536]{1,0:T(8,128)S(1)}, f32[384,1536]{1,0:T(8,128)}, u32[]{:S(2)}) copy-start(f32[384,1536]{1,0:T(8,128)} %get-tuple-element.1650) | copy-start | bytes 7077892
  2556.5 4.9 copy-start.10
  (7 other events, 7.3 us)
Sparse Core Ops, SparseCore 0:
  9.6 49.0 all-gather.9
  63.3 56.4 all-gather.13
  123.3 55.3 all-gather.11
  180.1 36.3 all-gather.15
  218.4 167.2 all-gather.17
  387.1 88.7 all-gather.19
  705.3 142.1 reduce-scatter.8
  849.8 138.0 reduce-scatter.6
  990.5 73.7 reduce-scatter.12
  1067.4 99.5 reduce-scatter.10
  1169.6 197.7 reduce-scatter.16
  1369.8 377.9 reduce-scatter.14
  1752.7 770.6 all-reduce.7
where the time goes:
time: 2580 us; the launch traced here: 2570 us
  waiting for transfers between devices  2040 us (79%)
  matrix products  280 us (11%)
  local copies, waits for them, and re-layouts  138 us (5%)
  blocking collectives  52.2 us (2%)
  other arithmetic  43.2 us (2%)
    psum x1, waiting for transfers between devices, body(): lax.psum((gain_one_shard, qkv_shard, bias_shard, out_shard), 'ctx')  720 us
    reduce_scatter x1, waiting for transfers between devices, body(): lax.psum_scatter(d_w_gate_up, 'fsdp', scatter_dimension=0, tiled=True)  380 us
    reduce_scatter x1, waiting for transfers between devices, body(): lax.psum_scatter(d_w_down, 'fsdp', scatter_dimension=0, tiled=True)  200 us
    reduce_scatter x1, waiting for transfers between devices, body(): lax.psum_scatter(by_device(buffers[0]), ('ctx', 'fsdp'), scatter_dimensio...  139 us
    all_gather x1, waiting for transfers between devices, body(): lax.all_gather(w_gate_up, 'fsdp', axis=0, tiled=True)  132 us
    reduce_scatter x1, waiting for transfers between devices, body(): lax.psum_scatter(by_device(buffers[1]), ('ctx', 'fsdp'), scatter_dimensio...  132 us
    reduce_scatter x1, waiting for transfers between devices, body(): lax.psum_scatter(d_w_qkv, 'fsdp', scatter_dimension=0, tiled=True)  103 us
    all_gather x1, waiting for transfers between devices, body(): lax.all_gather(w_down, 'fsdp', axis=0, tiled=True)  73.9 us
  transfers between devices with their start and end apart: 13, of which 12 were waited for; matrix products, arithmetic and copies ran while one was open for 7% of the time, Pallas kernels for 0%

commit v1 on v0

--- a/solution.py
+++ b/solution.py
@@ -179,7 +179,9 @@
     hidden = inputs + jnp.dot(attended16, w_out_full, preferred_element_type=f32)
     gain_two_w, w_gu_full, w_down_full = (
         lax.all_gather(gain_mlp, "fsdp", axis=0, tiled=True),
-        lax.all_gather(w_gate_up, "fsdp", axis=0, tiled=True),
+        jnp.concatenate(
+            lax.all_to_all(jnp.stack([w_gate_up] * lax.axis_size("fsdp")), "fsdp", 0, 0), axis=0
+        ),
         lax.all_gather(w_down, "fsdp", axis=0, tiled=True),
     )
     gain_two = gain_two_w.astype(f32)

time: 2580 us -> 2800 us (1.085)
  blocking collectives: 52.2 us -> 523 us
  waiting for transfers between devices: 2040 us -> 1740 us
  local copies, waits for them, and re-layouts: 138 us -> 168 us
    all_gather x1, blocking collectives: 5.18 us -> 476 us  [body(): lax.all_gather(gain_mlp, 'fsdp', axis=0, tiled=True)]
    all_gather x1, waiting for transfers between devices: 132 us -> 0.01 us  [body(): lax.all_gather(w_gate_up, 'fsdp', axis=0, tiled=True)]
    all_gather x1, waiting for transfers between devices: 73.9 us -> 0.01 us  [body(): lax.all_gather(w_down, 'fsdp', axis=0, tiled=True)]
    all_gather x1, waiting for transfers between devices: 55.6 us -> 0.02 us  [body(): lax.all_gather(key16.reshape(2, half_rows, kv_width), ('ctx', 'fsdp'), ax...]
    all_gather x1, waiting for transfers between devices: 35.4 us -> 0.02 us  [body(): lax.all_gather(value16.reshape(2, half_rows, kv_width), ('ctx', 'fsdp'),...]
  transfers between devices with their start and end apart: 13 -> 14, of which waited for: 12 -> 8; matrix products, arithmetic and copies ran while one was open for 7% -> 8% of each run, Pallas kernels for 0% -> 0%
where the time goes in v1:
time: 2800 us; the launch traced here: 2780 us
  waiting for transfers between devices  1740 us (62%)
  blocking collectives  523 us (19%)
  matrix products  278 us (10%)
  local copies, waits for them, and re-layouts  168 us (6%)
  other arithmetic  42.4 us (2%)
    psum x1, waiting for transfers between devices, body(): lax.psum((gain_one_shard, qkv_shard, bias_shard, out_shard), 'ctx')  720 us
    all_gather x1, blocking collectives, body(): lax.all_gather(gain_mlp, 'fsdp', axis=0, tiled=True)  476 us
    reduce_scatter x1, waiting for transfers between devices, body(): lax.psum_scatter(d_w_gate_up, 'fsdp', scatter_dimension=0, tiled=True)  380 us
    reduce_scatter x1, waiting for transfers between devices, body(): lax.psum_scatter(d_w_down, 'fsdp', scatter_dimension=0, tiled=True)  200 us
    reduce_scatter x1, waiting for transfers between devices, body(): lax.psum_scatter(by_device(buffers[0]), ('ctx', 'fsdp'), scatter_dimensio...  140 us
    reduce_scatter x1, waiting for transfers between devices, body(): lax.psum_scatter(by_device(buffers[1]), ('ctx', 'fsdp'), scatter_dimensio...  132 us
    reduce_scatter x1, waiting for transfers between devices, body(): lax.psum_scatter(d_w_qkv, 'fsdp', scatter_dimension=0, tiled=True)  103 us
    unnamed x102, local copies, waits for them, and re-layouts  58.7 us
  transfers between devices with their start and end apart: 14, of which 8 were waited for; matrix products, arithmetic and copies ran while one was open for 8% of the time, Pallas kernels for 0%

profile of v1, /device:TPU:0, one launch (start us, length us, event | category | flops | bytes accessed | tf_op | source)
XLA Modules:
  0.0 2782.8 jit_solution(6253447364450887504)
XLA Ops:
  8.7 6.2 all-gather
  16.8 5.5 all-gather.1
  22.5 36.2 %all-gather.10.cloned.1.call-done = bf16[1536,2048]{1,0:T(8,128)(2,1)} async-done(((bf16[384,2048]{1,0:T(8,128)(2,1)}), bf16[1536,2048]{1,0:T(8,128)(2,1)}) %all-gather.10.cloned.1.call-update) | async-done | bytes 6291472 | tf_op jit(solution)/shard_map/all_gather | solution.py:86
  58.7 3.8 convolution_add_fusion.2
  68.2 6.6 copy.165
  74.8 11.2 stack.37
  86.0 8.9 all-to-all-start
  96.5 476.0 %all-gather.2 = bf16[4,1,384]{2,1,0:T(2,128)(2,1)S(1)} all-gather(bf16[1,1,384]{2,1,0:T(2,128)(2,1)S(1)} %reshape.588), channel_id=1, replica_groups=mesh['ctx'=8,'fsdp'=4] {'fsdp'}, dimensions={0}, use_global_device_ids=true | all-gather | bytes 3840 | tf_op jit(solution)/shard_map/all_gather | solution.py:181
  574.8 2.8 fusion.182
  597.1 4.0 reshape.627
  601.1 3.2 copy.157
  604.3 13.9 while.80
  618.2 24.5 while.81
  649.3 3.4 multiply_reduce_fusion.2
  652.8 19.4 copy.166
  672.1 14.7 fusion.167
  686.9 11.8 fusion.149
  698.7 16.1 multiply_reduce_fusion
  716.2 4.3 convolution_convert_fusion
  727.8 7.9 while.82
  736.1 123.7 %while.83 = (s32[]{:T(128)}, f32[2,6,64,128]{3,2,1,0:T(8,128)S(1)}, f32[4096,2,128]{2,0,1:T(8,128)}, f32[4096,2,128]{2,0,1:T(8,128)}, s32[]{:T(128)}, /*index=5*...) while((s32[]{:T(128)}, f32[2,6,64,128]{3,2,1,0:T(8,128)S(1)}, ...), condition=%wide.region_21.23_spmd.clone, body=%wide.region_20.22_spmd.clone.sunk | while | flops 253641088 | bytes 6595315 | solution.py:288
  859.8 8.8 copy.216
  868.6 6.4 reshape.631
  875.0 8.8 copy.218
  883.8 6.4 reshape.632
  890.2 4.3 gather_fusion.5
  894.5 4.3 gather_fusion.7
  898.8 4.2 gather_fusion.4
  903.0 4.2 gather_fusion.6
  907.2 4.2 broadcast_select_fusion.2
  915.6 4.5 pad_maximum_fusion
  920.2 5.0 fusion.163
  926.3 132.1 %reduce-scatter.9.cloned.1.call-done = f32[2,64,256]{2,1,0:T(8,128)} async-done(((f32[2,2048,256]{2,1,0:T(8,128)}), f32[2,64,256]{2,1,0:T(8,128)}) %reduce-scatter.9.cloned.1.call-update) | async-done | bytes 131088 | tf_op jit(solution)/shard_map/reduce_scatter | solution.py:304
  1059.3 140.3 %reduce-scatter.7.cloned.1.call-done = f32[2,64,256]{2,1,0:T(8,128)} async-done(((f32[2,2048,256]{2,1,0:T(8,128)}), f32[2,64,256]{2,1,0:T(8,128)}) %reduce-scatter.7.cloned.1.call-update) | async-done | bytes 131088 | tf_op jit(solution)/shard_map/reduce_scatter | solution.py:303
  1201.3 8.6 fusion.176
  1210.9 14.8 fusion.145
  1227.0 23.1 fusion.143
  1250.4 25.7 reduce-scatter.13.cloned.1.call-done
  1276.1 102.6 %reduce-scatter.11.cloned.1.call-done = f32[384,2048]{1,0:T(8,128)} async-done(((f32[1536,2048]{1,0:T(8,128)}), f32[384,2048]{1,0:T(8,128)}) %reduce-scatter.11.cloned.1.call-update) | async-done | bytes 3145744 | tf_op jit(solution)/shard_map/reduce_scatter | solution.py:320
  1378.7 200.4 %reduce-scatter.17.cloned.1.call-done = f32[1120,1536]{1,0:T(8,128)} async-done(((f32[4480,1536]{1,0:T(8,128)}), f32[1120,1536]{1,0:T(8,128)}) %reduce-scatter.17.cloned.1.call-update) | async-done | bytes 6881296 | tf_op jit(solution)/shard_map/reduce_scatter | solution.py:216
  1579.1 380.5 %reduce-scatter.15.cloned.1.call-done = f32[384,2,4480]{2,0,1:T(8,128)} async-done(((f32[1536,2,4480]{2,0,1:T(8,128)}), f32[384,2,4480]{2,0,1:T(8,128)}) %reduce-scatter.15.cloned.1.call-update) | async-done | bytes 13762576 | tf_op jit(solution)/shard_map/reduce_scatter | solution.py:215
  1962.7 9.4 fusion.132
  1972.5 3.7 fusion.159
  1976.3 11.6 all-reduce.5
  1988.1 23.6 all-reduce.3
  2014.7 720.5 %all-reduce.8.cloned.1.call-done = (f32[384,2048]{1,0:T(8,128)}, f32[384,1536]{1,0:T(8,128)}, f32[384,2,4480]{2,0,1:T(8,128)}, f32[1120,1536]{1,0:T(8,128)}) async-done(((f32[384,2048]{1,0:T(8,128)}, f32[384,1536]{1,0:T(8,128)}, f32[384,2,4480]{2,0,1:T(8,128)}, f32[1120,1536]{1,0:T(8,128)}), (f32[384,2048]{1,0:T(8,128)}, f32[384,1536]{1,0:T(8,128)}, f32[384,2,4480]{2,0,1:T(8,128)}, ...) | async-done | bytes 26148880 | tf_op jit(solution)/shard_map/psum | solution.py:325
  2735.2 33.1 %copy.187 = f32[384,2,4480]{2,1,0:T(2,128)} copy(f32[384,2,4480]{2,0,1:T(8,128)} %get-tuple-element.961) | data formatting | bytes 27525120
  2773.2 2.9 copy.284
  (560 shorter events, 235.3 us)
Async XLA Ops:
  7.2 15.1 copy-start.5
  7.2 51.5 %all-gather.10.cloned.1.call-start = ((), (), s32[]{:S(2)}) async-start(), calls=%async_computation.7 | async-start | bytes 7864320 | tf_op jit(solution)/shard_map/all_gather | solution.py:86
  7.9 566.9 %all-gather.14.cloned.1.call-start = ((), (), s32[]{:S(2)}) async-start(), calls=%async_computation.9 | async-start | bytes 2162688 | tf_op jit(solution)/shard_map/all_gather | solution.py:107
  14.9 43.8 %copy-start.26 = (f32[1536]{0:T(1024)}, f32[1536]{0:T(1024)S(1)}, u32[]{:S(2)}) copy-start(f32[1536]{0:T(1024)S(1)} %reshape.590) | copy-start | bytes 18436
  16.1 42.6 %copy-start.32 = (f32[128]{0:T(128)}, f32[128]{0:T(128)S(1)}, u32[]{:S(2)}) copy-start(f32[128]{0:T(128)S(1)} %rsqrt.26) | copy-start | bytes 1540
  22.5 40.0 %copy-start.11 = (bf16[128,1536]{1,0:T(8,128)(2,1)}, bf16[128,1536]{1,0:T(8,128)(2,1)S(1)}, u32[]{:S(2)}) copy-start(bf16[128,1536]{1,0:T(8,128)(2,1)S(1)} %fusion.153) | copy-start | bytes 1179652
  58.7 4.5 copy-start.37
  63.1 515.1 %all-gather.12.cloned.1.call-start = ((), (), s32[]{:S(2)}) async-start(), calls=%async_computation.8 | async-start | bytes 2162688 | tf_op jit(solution)/shard_map/all_gather | solution.py:106
  65.6 2.6 copy-start.22
  65.7 2.5 copy-start.24
  66.9 582.3 %all-gather.16.cloned.1.call-start = ((), (), s32[]{:S(2)}) async-start(), calls=%async_computation.10 | async-start | bytes 5898240 | tf_op jit(solution)/shard_map/all_gather | solution.py:88
  67.5 619.4 %all-gather.18.cloned.1.call-start = ((), (), s32[]{:S(2)}) async-start(), calls=%async_computation.11 | async-start | bytes 17203200 | tf_op jit(solution)/shard_map/all_gather | solution.py:185
  68.1 630.6 %all-gather.20.cloned.1.call-start = ((), (), s32[]{:S(2)}) async-start(), calls=%async_computation.12 | async-start | bytes 34406400 | tf_op jit(solution)/shard_map/all_gather | solution.py:198
  86.0 10.5 copy-start.38
  86.0 566.8 %all-to-all-start = ((bf16[4,384,2,4480]{3,1,2,0:T(8,128)(2,1)}), bf16[4,384,2,4480]{3,1,2,0:T(8,128)(2,1)}, u32[]{:S(2)}, u32[]{:S(2)}) async-start(bf16[4,384,2,4480]{3,1,2,0:T(8,128)(2,1)} %stack.37), calls=%async_computation | async-start | bytes 55050240 | tf_op jit(solution)/shard_map/all_to_all | solution.py:183
  94.9 963.4 %reduce-scatter.9.cloned.1.call-start = ((), (), s32[]{:S(2)}) async-start(), calls=%async_computation.14 | async-start | bytes 4325376 | tf_op jit(solution)/shard_map/reduce_scatter | solution.py:304
  587.2 2.5 copy-start.13
  646.1 3.2 copy-start.4
  646.1 6.6 copy-start.30
  672.1 14.7 copy-start.18
  698.7 16.1 copy-start.20
  716.2 204.0 %copy-start.2 = (f32[128,1536]{1,0:T(8,128)}, f32[128,1536]{1,0:T(8,128)S(1)}, u32[]{:S(2)}) copy-start(f32[128,1536]{1,0:T(8,128)S(1)} %subtract_add_fusion) | copy-start | bytes 2359300
  727.8 8.3 copy-start.29
  903.0 4.2 copy-start.36
  907.2 4.2 copy-start.7
  907.2 4.2 copy-start.8
  907.2 4.2 copy-start.35
  915.6 284.1 %reduce-scatter.7.cloned.1.call-start = ((), (), s32[]{:S(2)}) async-start(), calls=%async_computation.13 | async-start | bytes 4325376 | tf_op jit(solution)/shard_map/reduce_scatter | solution.py:303
  920.2 355.9 %reduce-scatter.13.cloned.1.call-start = ((), (), s32[]{:S(2)}) async-start(), calls=%async_computation.16 | async-start | bytes 11796480 | tf_op jit(solution)/shard_map/reduce_scatter | solution.py:322
  925.2 453.5 %reduce-scatter.11.cloned.1.call-start = ((), (), s32[]{:S(2)}) async-start(), calls=%async_computation.15 | async-start | bytes 15728640 | tf_op jit(solution)/shard_map/reduce_scatter | solution.py:320
  925.8 274.9 %copy-start.23 = (f32[128,64]{1,0:T(8,128)S(1)}, f32[128,64]{1,0:T(8,128)}, u32[]{:S(2)}) copy-start(f32[128,64]{1,0:T(8,128)} %copy-done.22) | copy-start | bytes 98308
  925.8 274.9 %copy-start.25 = (f32[128,64]{1,0:T(8,128)S(1)}, f32[128,64]{1,0:T(8,128)}, u32[]{:S(2)}) copy-start(f32[128,64]{1,0:T(8,128)} %copy-done.24) | copy-start | bytes 98308
  926.1 275.2 %copy-start.12 = (bf16[128,1536]{1,0:T(8,128)(2,1)S(1)}, bf16[128,1536]{1,0:T(8,128)(2,1)}, u32[]{:S(2)}) copy-start(bf16[128,1536]{1,0:T(8,128)(2,1)} %copy-done.11) | copy-start | bytes 1179652
  926.2 283.6 %copy-start = (f32[128,12,128]{0,2,1:T(8,128)}, f32[128,12,128]{0,2,1:T(8,128)S(1)}, u32[]{:S(2)}) copy-start(f32[128,12,128]{0,2,1:T(8,128)S(1)} %pad_maximum_fusion.8) | copy-start | bytes 2359300
  1209.9 369.2 %reduce-scatter.17.cloned.1.call-start = ((), (), s32[]{:S(2)}) async-start(), calls=%async_computation.18 | async-start | bytes 34406400 | tf_op jit(solution)/shard_map/reduce_scatter | solution.py:216
  1225.7 733.9 %reduce-scatter.15.cloned.1.call-start = ((), (), s32[]{:S(2)}) async-start(), calls=%async_computation.17 | async-start | bytes 68812800 | tf_op jit(solution)/shard_map/reduce_scatter | solution.py:215
  1250.1 1485.0 %all-reduce.8.cloned.1.call-start = ((), (), s32[]{:S(2)}) async-start(), calls=%async_computation.19 | async-start | bytes 52297728 | tf_op jit(solution)/shard_map/psum | solution.py:325
  1959.6 2.5 copy-start.33
  1959.6 12.8 slice-start
  1962.7 9.4 copy-start.1
  1962.7 9.8 slice-start.1
  1962.7 9.8 copy-start.6
  1962.7 9.8 copy-start.27
  1962.7 9.8 copy-start.34
  1972.5 39.8 %copy-start.3 = (f32[128,1536]{1,0:T(8,128)S(1)}, f32[128,1536]{1,0:T(8,128)}, u32[]{:S(2)}) copy-start(f32[128,1536]{1,0:T(8,128)} %copy-done.2) | copy-start | bytes 2359300
  2735.2 33.1 %copy-start.16 = (f32[384,2048]{1,0:T(8,128)S(1)}, f32[384,2048]{1,0:T(8,128)}, u32[]{:S(2)}) copy-start(f32[384,2048]{1,0:T(8,128)} %get-tuple-element.1648) | copy-start | bytes 9437188
  2735.2 34.8 %copy-start.17 = (f32[384,1536]{1,0:T(8,128)S(1)}, f32[384,1536]{1,0:T(8,128)}, u32[]{:S(2)}) copy-start(f32[384,1536]{1,0:T(8,128)} %get-tuple-element.1650) | copy-start | bytes 7077892
  2768.2 4.9 copy-start.10
  (8 other events, 12.3 us)
Sparse Core Ops, SparseCore 0:
  9.6 49.0 all-gather.9
  63.3 58.7 all-gather.13
  125.5 58.0 all-gather.11
  185.0 61.7 all-gather.15
  248.2 162.5 all-gather.17
  412.9 237.7 all-gather.19
  915.7 142.5 reduce-scatter.8
  1061.2 138.4 reduce-scatter.6
  1202.2 73.7 reduce-scatter.12
  1279.1 99.5 reduce-scatter.10
  1381.3 197.7 reduce-scatter.16
  1581.6 377.9 reduce-scatter.14
  1964.5 770.6 all-reduce.7
